TPU v7x, 32 devices: a whole 2x2x4 slice. The times are simulated.
32 devices in a mesh: section: 4 (over z), ctx: 8 (over y, x, core).
Axes of the slice: x: 2, y: 2, z: 4, core: 2. Of those that a mesh axis runs over, the one named last changes fastest.
Arguments:
- queries: bfloat16 [4, 1024, 4096], P('section', 'ctx'), may hold values from -130 to 130
- keys_new: bfloat16 [4, 1024, 1024], P('section', 'ctx'), may hold values from -6 to 6
- values_new: bfloat16 [4, 1024, 1024], P('section', 'ctx'), may hold values from -6 to 6
- stretch_cache: bfloat16 [4, 512, 2048], P('section'), may hold values from -6 to 6
- hadamard_signs: int32 [4, 2, 128], P('section'), may hold values from -1 to 1, as said below
- stretch_docs: int32 [8], replicated, may hold values from 0 to 1, never falling along the last dimension, each value on 1 to 5 neighbouring positions
Outputs:
- handed: bfloat16 [4, 1024, 4096], P('section', 'ctx')
Inputs may be any that keep to these rules, and one draw needn't show every extreme that they name: `hadamard_signs`: each entry is -1 or 1. `stretch_docs`: never falling along the stretches; each document covers 1 to 5 stretches in a row.
All inputs are finite; a program needn't handle non-finite values.
Results may differ from a plain program's by a relative error of at most 0.0099.
Values may be sent and summed in bfloat16 or wider, within the bound.
A program may use at most 128 MiB of HBM per device.

v0:
```python
import functools

import jax
import jax.numpy as jnp
import numpy as np
from jax import lax
from jax.experimental import pallas as pl
from jax.experimental.pallas import tpu as pltpu
from jax.sharding import PartitionSpec as P

CACHE = 256
MESH = pl.DeviceIdType.MESH


def hadamard(length):
    numbers = np.arange(length)
    common = numbers[:, None] & numbers[None, :]
    parity = np.zeros((length, length), np.int64)
    for bit_place in range(max(int(length).bit_length(), 1)):
        parity = parity ^ common >> bit_place & 1
    return 1.0 - 2.0 * parity


def attention_kernel(
    n,
    sections,
    docs_ref,
    signs_ref,
    hada_ref,
    q_hbm,
    k_hbm,
    v_hbm,
    cache_hbm,
    out_hbm,
    q_buf,
    cache_buf,
    own,
    held,
    out_buf,
    load_sem,
    own_sem,
    send_sem,
    recv_sem,
    out_send,
    out_recv,
):
    section = lax.axis_index("section")
    me = lax.axis_index("ctx")
    odd = lax.rem(me, 2)
    reach = held.shape[0]
    half = reach // 2
    heads = own.shape[0]
    rows, hd = own.shape[2], own.shape[3]
    width = out_buf.shape[2]
    groups = width // hd
    kv_width = heads * hd
    detour = n == 8

    def cols(start, size):
        return pl.ds(pl.multiple_of(start, hd), size)

    def own_copies(h):
        return (
            pltpu.make_async_copy(k_hbm.at[:, cols(h * hd, hd)], own.at[h, 0], own_sem.at[h, 0]),
            pltpu.make_async_copy(v_hbm.at[:, cols(h * hd, hd)], own.at[h, 1], own_sem.at[h, 1]),
        )

    def start_own(h, carry):
        for copy in own_copies(h):
            copy.start()
        return carry

    lax.fori_loop(0, heads, start_own, 0)
    cache_copy = pltpu.make_async_copy(cache_hbm, cache_buf, load_sem.at[0])
    cache_copy.start()
    q_copy = pltpu.make_async_copy(q_hbm, q_buf, load_sem.at[1])
    q_copy.start()

    barrier = pltpu.get_barrier_semaphore()
    sibling = me + 1 - 2 * odd
    following = lax.rem(section + 1, sections)
    previous = lax.rem(section + sections - 1, sections)

    def greet(sec, ctx):
        pl.semaphore_signal(barrier, inc=1, device_id=(sec, ctx), device_id_type=MESH)

    greet(section, sibling)
    greet(following, me)
    greet(previous, me)
    count = jnp.int32(3)
    for e in range(2, reach + 1, 2):
        @pl.when(me + e < n)
        def _(e=e):
            greet(section, me + e)

        @pl.when(me >= e)
        def _(e=e):
            greet(section, me - e)

        count = count + jnp.where(me + e < n, 1, 0) + jnp.where(me >= e, 1, 0)
    pl.semaphore_wait(barrier, count)

    def remote(src, row, h, target, distance):
        return pltpu.make_async_remote_copy(
            src_ref=src,
            dst_ref=held.at[distance - 1, h],
            send_sem=send_sem.at[row, h],
            recv_sem=recv_sem.at[distance - 1, h],
            device_id=(section, target),
            device_id_type=MESH,
        )

    def own_sends(h, act):
        for e in range(2, reach + 1, 2):
            go = me + e < n
            if detour and e == 2:
                go = go & (me // 2 != 1)

            @pl.when(go)
            def _(e=e):
                act(remote(own.at[h], e // 2 - 1, h, me + e, e))

        @pl.when(odd == 0)
        def _():
            act(remote(own.at[h], half, h, me + 1, 1))

    def relay_sends(h, act, wait):
        for e in range(reach, 1, -2):
            @pl.when(me >= e)
            def _(e=e):
                block = held.at[e - 1, h]
                if wait:
                    remote(block, 0, h, me, e).wait_recv()
                if detour and e == 4:
                    @pl.when(me >= n - 2)
                    def _():
                        act(remote(block, reach + 1, h, me - 2, 2))

                @pl.when(odd == 1)
                def _():
                    act(remote(block, half + e // 2, h, me - 1, e - 1))

                if e < reach:
                    @pl.when(odd == 0)
                    def _():
                        act(remote(block, half + e // 2, h, me + 1, e + 1))

    def send_own(h, carry):
        for copy in own_copies(h):
            copy.wait()
        own_sends(h, lambda copy: copy.start())
        return carry

    lax.fori_loop(0, heads, send_own, 0)

    for d in range(1, reach + 1):
        @pl.when(me < d)
        def _(d=d):
            held[d - 1] = jnp.zeros(held.shape[1:], held.dtype)

    my_doc = docs_ref[me]
    biases = []
    for d in range(1, reach + 1):
        seen = (me >= d) & (docs_ref[jnp.maximum(me - d, 0)] == my_doc)
        biases.append(jnp.where(seen, 0.0, -jnp.inf).astype(jnp.float32))
    picks = [
        jnp.full((1, hd), jnp.where(my_doc == doc, 1.0, 0.0), jnp.float32).astype(jnp.bfloat16)
        for doc in range(cache_buf.shape[0] // CACHE)
    ]

    def cache_block(start):
        terms = [
            cache_buf[doc * CACHE : (doc + 1) * CACHE, cols(start, hd)] * pick
            for doc, pick in enumerate(picks)
        ]
        return functools.reduce(jnp.add, terms)

    root = hd ** -0.5
    sign_k = signs_ref[0:1, :].astype(jnp.float32) * root
    sign_v = signs_ref[1:2, :].astype(jnp.float32) * root
    hada = hada_ref[...]
    factor = root * float(np.log2(np.e))
    cache_copy.wait()
    q_copy.wait()
    relay_sends(0, lambda copy: copy.start(), True)

    def out_copy(h):
        return pltpu.make_async_remote_copy(
            src_ref=out_buf.at[h],
            dst_ref=out_hbm.at[:, cols(h * width, width)],
            send_sem=out_send.at[h],
            recv_sem=out_recv.at[h],
            device_id=(following, me),
            device_id_type=MESH,
        )

    causal = lax.broadcasted_iota(jnp.int32, (rows, rows), 1) <= lax.broadcasted_iota(
        jnp.int32, (rows, rows), 0
    )

    def head_step(h, carry):
        back_k = jnp.dot(cache_block(h * hd), hada, preferred_element_type=jnp.float32)
        back_v = jnp.dot(cache_block(kv_width + h * hd), hada, preferred_element_type=jnp.float32)
        back_k = (back_k * sign_k).astype(jnp.bfloat16)
        back_v = (back_v * sign_v).astype(jnp.bfloat16)
        for d in range(1, reach + 1, 2):
            @pl.when(me >= d)
            def _(d=d):
                remote(held.at[d - 1, h], 0, h, me, d).wait_recv()
        keys = jnp.concatenate(
            [back_k, own[h, 0]] + [held[d, h, 0] for d in range(reach)], axis=0
        )
        values = jnp.concatenate(
            [back_v, own[h, 1]] + [held[d, h, 1] for d in range(reach)], axis=0
        )
        for g in range(groups):
            if g == groups // 2:
                @pl.when(h + 1 < heads)
                def _():
                    relay_sends(h + 1, lambda copy: copy.start(), True)
            query = q_buf[:, cols(h * width + g * hd, hd)]
            scores = lax.dot_general(
                query, keys, (((1,), (1,)), ((), ())), preferred_element_type=jnp.float32
            )
            parts = [scores[:, at : at + rows] for at in range(0, CACHE, rows)]
            parts.append(jnp.where(causal, scores[:, CACHE : CACHE + rows], -jnp.inf))
            for d in range(reach):
                at = CACHE + rows * (d + 1)
                parts.append(scores[:, at : at + rows] + biases[d])
            top = functools.reduce(jnp.maximum, parts)
            top = jnp.max(top, axis=1, keepdims=True)
            expo = [jnp.exp2((part - top) * factor) for part in parts]
            total = jnp.sum(functools.reduce(jnp.add, expo), axis=1, keepdims=True)
            weights = jnp.concatenate([part.astype(jnp.bfloat16) for part in expo], axis=1)
            summed = jnp.dot(weights, values, preferred_element_type=jnp.float32)
            out_buf[h, :, g * hd : (g + 1) * hd] = (summed / total).astype(out_buf.dtype)
        out_copy(h).start()
        return carry

    lax.fori_loop(0, heads, head_step, 0)

    def finish(h, carry):
        own_sends(h, lambda copy: copy.wait_send())
        relay_sends(h, lambda copy: copy.wait_send(), False)
        out_copy(h).wait()
        return carry

    lax.fori_loop(0, heads, finish, 0)


def per_device(n, sections, queries, keys_new, values_new, stretch_cache, signs, docs):
    rows, q_width = queries.shape[1:]
    kv_width = keys_new.shape[-1]
    hd = signs.shape[-1]
    heads = kv_width // hd
    width = q_width // heads
    reach = n // 2
    dtype = queries.dtype
    anywhere = pl.BlockSpec(memory_space=pl.ANY)
    vmem = pl.BlockSpec(memory_space=pltpu.VMEM)
    out = pl.pallas_call(
        functools.partial(attention_kernel, n, sections),
        out_shape=jax.ShapeDtypeStruct((rows, q_width), dtype),
        in_specs=[pl.BlockSpec(memory_space=pltpu.SMEM), vmem, vmem] + [anywhere] * 4,
        out_specs=anywhere,
        scratch_shapes=[
            pltpu.VMEM((rows, q_width), dtype),
            pltpu.VMEM(stretch_cache.shape[1:], dtype),
            pltpu.VMEM((heads, 2, rows, hd), dtype),
            pltpu.VMEM((reach, heads, 2, rows, hd), dtype),
            pltpu.VMEM((heads, rows, width), dtype),
            pltpu.SemaphoreType.DMA((2,)),
            pltpu.SemaphoreType.DMA((heads, 2)),
            pltpu.SemaphoreType.DMA((reach + 2, heads)),
            pltpu.SemaphoreType.DMA((reach, heads)),
            pltpu.SemaphoreType.DMA((heads,)),
            pltpu.SemaphoreType.DMA((heads,)),
        ],
        compiler_params=pltpu.CompilerParams(
            collective_id=0, has_side_effects=True, vmem_limit_bytes=60 * 1024 * 1024
        ),
    )(
        docs,
        signs[0],
        jnp.asarray(hadamard(hd), dtype),
        queries[0],
        keys_new[0],
        values_new[0],
        stretch_cache[0],
    )
    return out[None]


def solution(mesh):
    in_specs = (
        P("section", "ctx", None),
        P("section", "ctx", None),
        P("section", "ctx", None),
        P("section", None, None),
        P("section", None, None),
        P(),
    )
    out_specs = P("section", "ctx", None)
    body = functools.partial(per_device, mesh.shape["ctx"], mesh.shape["section"])
    return jax.shard_map(body, mesh=mesh, in_specs=in_specs, out_specs=out_specs, check_vma=False)
```

profile of v0, /device:TPU:4, one launch (start us, length us, event | category | flops | bytes accessed | tf_op | source)
XLA Modules:
  0.0 43.0 jit_solution(5691947771040914473)
XLA Ops:
  0.0 40.7 %shard_map.73 = bf16[128,4096]{1,0:T(8,128)(2,1)} custom-call(s32[8]{0:T(128)} %docs_ref.1, s32[2,128]{1,0:T(2,128)} %bitcast.11, bf16[128,128]{1,0:T(8,128)(2,1)} %constant.2.clone.hada_ref, bf16[128,4096]{1,0:T(8,128)(2,1)} %bitcast.8, bf16[128,1024]{1,0:T(8,128)(2,1)} %bitcast.9, bf16[128,1024]{1,0:T(8,128)(2,1)} %bitcast.10, bf16[512,2048]{1,0:T(8,128)(2,1)} %bitcast.7), custom_call_target="tpu_custom_call" | custom-call | tf_op jit(solution)/shard_map/pallas_call | solution.py:261
  40.7 2.3 %copy.9 = bf16[1,128,4096]{2,1,0:T(8,128)(2,1)} copy(bf16[1,128,4096]{2,1,0:T(8,128)(2,1)} %bitcast.6) | data formatting | bytes 2097152
where the time goes:
time: 43.2 us; the launch traced here: 43 us
  Pallas kernels  40.7 us (94%)
  local copies, waits for them, and re-layouts  2.29 us (5%)
    pallas_call x1, Pallas kernels, per_device(): pl.pallas_call(functools.partial(attention_kernel, n, sections), out_shap...  40.7 us
    unnamed x1, local copies, waits for them, and re-layouts  2.29 us

commit v1 on v0

v1 whole, which is shorter than its diff:
```python
import functools

import jax
import jax.numpy as jnp
import numpy as np
from jax import lax
from jax.experimental import pallas as pl
from jax.experimental.pallas import tpu as pltpu
from jax.sharding import PartitionSpec as P

CACHE = 256
MESH = pl.DeviceIdType.MESH


def attention_kernel(
    n,
    sections,
    docs_hbm,
    signs_hbm,
    q_hbm,
    k_hbm,
    v_hbm,
    cache_hbm,
    out_ref,
    docs_ref,
    signs_ref,
    q_buf,
    q_send,
    cache_buf,
    own,
    held,
    out_buf,
    small_sem,
    cache_sem,
    q_sem,
    swap_send,
    swap_recv,
    own_sem,
    mine_sem,
    send_sem,
    recv_sem,
    out_send,
    out_recv,
    first_send,
    first_recv,
):
    section = lax.axis_index("section")
    me = lax.axis_index("ctx")
    p = lax.rem(me, 2)
    chip = me // 2
    chips = n // 2
    heads, hd = held.shape[0], held.shape[4]
    rows = held.shape[3]
    slots = held.shape[2]
    back = (slots - 2) // 2
    width = out_buf.shape[3]
    groups = width // hd
    all_heads = 2 * heads
    kv_width = all_heads * hd
    detour = chips == 4
    sibling = me + 1 - 2 * p
    following = lax.rem(section + 1, sections)
    previous = lax.rem(section + sections - 1, sections)

    def cols(start, size):
        return pl.ds(pl.multiple_of(start, hd), size)

    barrier = pltpu.get_barrier_semaphore()

    def greet(sec, ctx):
        pl.semaphore_signal(barrier, inc=1, device_id=(sec, ctx), device_id_type=MESH)

    for d in range(back, 0, -1):
        @pl.when(chip >= d)
        def _(d=d):
            greet(section, 2 * (chip - d))
            greet(section, 2 * (chip - d) + 1)
    greet(previous, 2 * chip)
    greet(previous, 2 * chip + 1)
    greet(section, sibling)

    def own_copies(h):
        return (
            pltpu.make_async_copy(k_hbm.at[:, cols(h * hd, hd)], own.at[h, 0], own_sem.at[h, 0]),
            pltpu.make_async_copy(v_hbm.at[:, cols(h * hd, hd)], own.at[h, 1], own_sem.at[h, 1]),
        )

    def mine_copies(i):
        h = p * heads + i
        slot = slots - 2 + p
        return (
            pltpu.make_async_copy(
                k_hbm.at[:, cols(h * hd, hd)], held.at[i, 0, slot], mine_sem.at[i, 0]
            ),
            pltpu.make_async_copy(
                v_hbm.at[:, cols(h * hd, hd)], held.at[i, 1, slot], mine_sem.at[i, 1]
            ),
        )

    def q_copies(i):
        theirs = (1 - p) * heads + i
        ours = p * heads + i
        return (
            pltpu.make_async_copy(
                q_hbm.at[:, cols(theirs * width, width)], q_send.at[i], q_sem.at[i, 0]
            ),
            pltpu.make_async_copy(
                q_hbm.at[:, cols(ours * width, width)], q_buf.at[p, i], q_sem.at[i, 1]
            ),
        )

    def cache_copies(i):
        h = p * heads + i
        return (
            pltpu.make_async_copy(
                cache_hbm.at[:, cols(h * hd, hd)], cache_buf.at[i, 0], cache_sem.at[i, 0]
            ),
            pltpu.make_async_copy(
                cache_hbm.at[:, cols(kv_width + h * hd, hd)], cache_buf.at[i, 1], cache_sem.at[i, 1]
            ),
        )

    def start_own(i, carry):
        for copy in own_copies(i) + own_copies(heads + i):
            copy.start()
        return carry

    def start_loads(i, carry):
        for copy in mine_copies(i) + cache_copies(i) + q_copies(i):
            copy.start()
        return carry

    small = (
        pltpu.make_async_copy(docs_hbm, docs_ref, small_sem.at[0]),
        pltpu.make_async_copy(signs_hbm, signs_ref, small_sem.at[1]),
    )
    start_own(0, 0)
    for copy in small:
        copy.start()
    start_loads(0, 0)
    lax.fori_loop(1, heads, start_own, 0)
    lax.fori_loop(1, heads, start_loads, 0)

    for d in range(1, back + 1):
        @pl.when(chip < d)
        def _(d=d):
            for i in range(heads):
                at = slots - 2 - 2 * d
                held[i, :, at : at + 2] = jnp.zeros((2, 2, rows, hd), held.dtype)

    low = lax.broadcasted_iota(jnp.int32, (hd, hd), 0) & lax.broadcasted_iota(
        jnp.int32, (hd, hd), 1
    )
    shift = 1
    while 2 * shift < hd:
        shift *= 2
    while shift:
        low = low ^ (low >> shift)
        shift //= 2
    hada = (1 - 2 * (low & 1)).astype(jnp.float32).astype(jnp.bfloat16)

    count = jnp.int32(3)
    for d in range(1, back + 1):
        count = count + jnp.where(chip + d < chips, 2, 0)
    pl.semaphore_wait(barrier, count)

    def remote(src, i, kind, slot, index, target):
        return pltpu.make_async_remote_copy(
            src_ref=src,
            dst_ref=held.at[i, kind, slot],
            send_sem=send_sem.at[index, i, kind],
            recv_sem=recv_sem.at[i, kind, slot],
            device_id=(section, target),
            device_id_type=MESH,
        )

    def swap_q(i):
        return pltpu.make_async_remote_copy(
            src_ref=q_send.at[i],
            dst_ref=q_buf.at[p, i],
            send_sem=swap_send.at[i],
            recv_sem=swap_recv.at[i],
            device_id=(section, sibling),
            device_id_type=MESH,
        )

    def start_swap_q(i):
        q_copies(i)[0].wait()
        swap_q(i).start()

    def swap_kv(i, kind):
        return remote(own.at[(1 - p) * heads + i, kind], i, kind, slots - 2 + p, 0, sibling)

    def ahead(i, act):
        for core in range(2):
            for kind in range(2):
                for d in range(1, back + 1):
                    go = chip + d < chips
                    if detour and d == 1:
                        go = go & (chip != 1)

                    @pl.when(go)
                    def _(core=core, kind=kind, d=d):
                        act(
                            remote(
                                own.at[core * heads + i, kind],
                                i,
                                kind,
                                slots - 2 - 2 * d + p,
                                2 * d - 1 + core,
                                2 * (chip + d) + core,
                            )
                        )

    def relays(i, act):
        if detour:
            @pl.when(chip == chips - 1)
            def _():
                for kind in range(2):
                    for slot in range(2):
                        act(
                            remote(
                                held.at[i, kind, slot], i, kind, slot + 2, 1 + slot, me - 2
                            ),
                            kind,
                            slot,
                        )

    def relay(i):
        def act(copy, kind, slot):
            arrived(i, kind, slot)
            copy.start()

        relays(i, act)

    def arrived(i, kind, slot):
        remote(own.at[0, kind], i, kind, slot, 0, sibling).wait_recv()

    def earlier(i, kind, slot):
        there = chip - back + slot // 2 >= 0
        if detour and slot < 2:
            there = there & (chip != chips - 1)

        @pl.when(there)
        def _():
            arrived(i, kind, slot)

    def send(i, carry):
        for copy in own_copies(i) + own_copies(heads + i):
            copy.wait()
        ahead(i, lambda copy: copy.start())
        for kind in range(2):
            swap_kv(i, kind).start()
        return carry

    lax.fori_loop(0, heads, send, 0)
    start_swap_q(0)

    for copy in small:
        copy.wait()
    root = hd ** -0.5
    sign_k = signs_ref[0:1, :].astype(jnp.float32) * root
    sign_v = signs_ref[1:2, :].astype(jnp.float32) * root
    factor = root * float(np.log2(np.e))
    causal = lax.broadcasted_iota(jnp.int32, (rows, rows), 1) <= lax.broadcasted_iota(
        jnp.int32, (rows, rows), 0
    )

    def out_copy(i, e):
        return pltpu.make_async_remote_copy(
            src_ref=out_buf.at[i, e],
            dst_ref=out_ref.at[:, cols((p * heads + i) * width, width)],
            send_sem=out_send.at[i, e],
            recv_sem=out_recv.at[p * heads + i],
            device_id=(following, 2 * chip + e),
            device_id_type=MESH,
        )

    def first_copy(g):
        return pltpu.make_async_remote_copy(
            src_ref=out_buf.at[0, p, :, g * hd : (g + 1) * hd],
            dst_ref=out_ref.at[:, cols(p * heads * width + g * hd, hd)],
            send_sem=first_send.at[g],
            recv_sem=first_recv.at[g],
            device_id=(following, me),
            device_id_type=MESH,
        )

    def step(t, carry):
        i = t // 2
        half = lax.rem(t, 2)
        e = (p + half) - 2 * p * half

        @pl.when(half == 0)
        def _():
            for copy in cache_copies(i):
                copy.wait()

            @pl.when(i + 1 < heads)
            def _():
                start_swap_q(i + 1)

        stretch = 2 * chip + e
        doc = docs_ref[stretch]
        picks = [
            jnp.full((1, hd), jnp.where(doc == k, 1.0, 0.0), jnp.float32).astype(jnp.bfloat16)
            for k in range(cache_buf.shape[2] // CACHE)
        ]

        def cache_block(kind):
            terms = [
                cache_buf[i, kind, k * CACHE : (k + 1) * CACHE, :] * pick
                for k, pick in enumerate(picks)
            ]
            return functools.reduce(jnp.add, terms)

        back_k = jnp.dot(cache_block(0), hada, preferred_element_type=jnp.float32)
        back_v = jnp.dot(cache_block(1), hada, preferred_element_type=jnp.float32)
        back_k = (back_k * sign_k).astype(jnp.bfloat16)
        back_v = (back_v * sign_v).astype(jnp.bfloat16)
        biases = []
        for d in range(slots - 2, 0, -1):
            seen = (stretch >= d) & (docs_ref[jnp.maximum(stretch - d, 0)] == doc)
            biases.append(jnp.where(seen, 0.0, -jnp.inf).astype(jnp.float32))

        def waits(kind):
            sibling_slot = slots - 1 - p
            first = half == 0

            @pl.when(first)
            def _():
                mine_copies(i)[kind].wait()
                for slot in range(1, slots - 2):
                    earlier(i, kind, slot)

            @pl.when(e == 0)
            def _():
                earlier(i, kind, 0)

            @pl.when(e == 1)
            def _():
                arrived(i, kind, sibling_slot)

        @pl.when(half == 0)
        def _():
            q_copies(i)[1].wait()

        @pl.when(half == 1)
        def _():
            swap_q(i).wait_recv()

        waits(0)
        waits(1)
        span = (slots - 1) * rows
        keys = held[i, 0, pl.ds(e, slots - 1)].reshape(span, hd)
        values = held[i, 1, pl.ds(e, slots - 1)].reshape(span, hd)
        keys = jnp.concatenate([back_k, keys], axis=0)
        values = jnp.concatenate([back_v, values], axis=0)
        for g in range(groups):
            query = q_buf[e, i, :, g * hd : (g + 1) * hd]
            scores = lax.dot_general(
                query, keys, (((1,), (1,)), ((), ())), preferred_element_type=jnp.float32
            )
            parts = [scores[:, at : at + rows] for at in range(0, CACHE, rows)]
            for d in range(slots - 2):
                at = CACHE + rows * d
                parts.append(scores[:, at : at + rows] + biases[d])
            parts.append(jnp.where(causal, scores[:, CACHE + span - rows :], -jnp.inf))
            top = functools.reduce(jnp.maximum, parts)
            top = jnp.max(top, axis=1, keepdims=True)
            expo = [jnp.exp2((part - top) * factor) for part in parts]
            total = jnp.sum(functools.reduce(jnp.add, expo), axis=1, keepdims=True)
            weights = jnp.concatenate([part.astype(jnp.bfloat16) for part in expo], axis=1)
            summed = jnp.dot(weights, values, preferred_element_type=jnp.float32)
            out_buf[i, e, :, g * hd : (g + 1) * hd] = (summed / total).astype(out_buf.dtype)

            @pl.when(t == 0)
            def _(g=g):
                first_copy(g).start()

        @pl.when(t > 0)
        def _():
            out_copy(i, e).start()

        @pl.when((half == 1) & (i + 1 < heads))
        def _():
            relay(i + 1)

        return carry

    relay(0)
    lax.fori_loop(0, 2 * heads, step, 0)

    def finish(i, carry):
        ahead(i, lambda copy: copy.wait_send())
        relays(i, lambda copy, kind, slot: copy.wait_send())
        for kind in range(2):
            swap_kv(i, kind).wait_send()
        swap_q(i).wait_send()
        return carry

    lax.fori_loop(0, heads, finish, 0)
    for g in range(groups):
        first_copy(g).wait_send()

    def sent(t, carry):
        half = lax.rem(t, 2)
        out_copy(t // 2, (p + half) - 2 * p * half).wait_send()
        return carry

    lax.fori_loop(1, 2 * heads, sent, 0)

    def received(core, i):
        return pltpu.make_async_remote_copy(
            src_ref=out_buf.at[i, 0],
            dst_ref=out_ref.at[:, cols((core * heads + i) * width, width)],
            send_sem=out_send.at[i, 0],
            recv_sem=out_recv.at[core * heads + i],
            device_id=(following, me),
            device_id_type=MESH,
        )

    for g in range(groups):
        first_copy(g).wait_recv()
    received(1 - p, 0).wait_recv()
    for i in range(1, heads):
        for core in range(2):
            received(core, i).wait_recv()


def per_device(n, sections, queries, keys_new, values_new, stretch_cache, signs, docs):
    rows, q_width = queries.shape[1:]
    kv_width = keys_new.shape[-1]
    hd = signs.shape[-1]
    all_heads = kv_width // hd
    heads = all_heads // 2
    width = q_width // all_heads
    groups = width // hd
    reach = n // 2
    slots = reach + 2
    cached = stretch_cache.shape[1]
    dtype = queries.dtype
    dma = pltpu.SemaphoreType.DMA
    in_hbm = pl.BlockSpec(memory_space=pltpu.HBM)
    out = pl.pallas_call(
        functools.partial(attention_kernel, n, sections),
        out_shape=pltpu.VMEM((rows, q_width), dtype),
        in_specs=[in_hbm] * 6,
        out_specs=pl.BlockSpec(memory_space=pltpu.VMEM),
        scratch_shapes=[
            pltpu.SMEM(docs.shape, docs.dtype),
            pltpu.VMEM(signs.shape[1:], signs.dtype),
            pltpu.VMEM((2, heads, rows, width), dtype),
            pltpu.VMEM((heads, rows, width), dtype),
            pltpu.VMEM((heads, 2, cached, hd), dtype),
            pltpu.VMEM((all_heads, 2, rows, hd), dtype),
            pltpu.VMEM((heads, 2, slots, rows, hd), dtype),
            pltpu.VMEM((heads, 2, rows, width), dtype),
            dma((2,)),
            dma((heads, 2)),
            dma((heads, 2)),
            dma((heads,)),
            dma((heads,)),
            dma((all_heads, 2)),
            dma((heads, 2)),
            dma((reach + 1, heads, 2)),
            dma((heads, 2, slots)),
            dma((heads, 2)),
            dma((all_heads,)),
            dma((groups,)),
            dma((groups,)),
        ],
        compiler_params=pltpu.CompilerParams(
            collective_id=0, has_side_effects=True, vmem_limit_bytes=58 * 1024 * 1024
        ),
    )(docs, signs[0], queries[0], keys_new[0], values_new[0], stretch_cache[0])
    return out[None]


def solution(mesh):
    in_specs = (
        P("section", "ctx", None),
        P("section", "ctx", None),
        P("section", "ctx", None),
        P("section", None, None),
        P("section", None, None),
        P(),
    )
    out_specs = P("section", "ctx", None)
    body = functools.partial(per_device, mesh.shape["ctx"], mesh.shape["section"])
    return jax.shard_map(body, mesh=mesh, in_specs=in_specs, out_specs=out_specs, check_vma=False)
```

time: 43.2 us -> 41.4 us (0.958)
  local copies, waits for them, and re-layouts: 2.29 us -> 0.97 us
  Pallas kernels: 40.7 us -> 39.9 us
    unnamed x1, local copies, waits for them, and re-layouts: 2.29 us -> 0.97 us
    pallas_call x1, Pallas kernels: 40.7 us -> 39.9 us  [per_device(): pl.pallas_call(functools.partial(attention_kernel, n, sections), out_shap...]
where the time goes in v1:
time: 41.4 us; the launch traced here: 40.9 us
  Pallas kernels  39.9 us (96%)
  local copies, waits for them, and re-layouts  0.97 us (2%)
    pallas_call x1, Pallas kernels, per_device(): pl.pallas_call(functools.partial(attention_kernel, n, sections), out_shap...  39.9 us
    unnamed x1, local copies, waits for them, and re-layouts  0.97 us

profile of v1, /device:TPU:4, one launch (start us, length us, event | category | flops | bytes accessed | tf_op | source)
XLA Modules:
  0.0 40.9 jit_solution(5830932687556903105)
XLA Ops:
  0.0 39.9 %shard_map.64 = bf16[128,4096]{1,0:T(8,128)(2,1)S(1)} custom-call(s32[8]{0:T(128)} %docs_hbm.1, s32[2,128]{1,0:T(2,128)} %bitcast.11, bf16[128,4096]{1,0:T(8,128)(2,1)} %bitcast.8, bf16[128,1024]{1,0:T(8,128)(2,1)} %bitcast.9, bf16[128,1024]{1,0:T(8,128)(2,1)} %bitcast.10, bf16[512,2048]{1,0:T(8,128)(2,1)} %bitcast.7), custom_call_target="tpu_custom_call" | custom-call | tf_op jit(solution)/shard_map/pallas_call | solution.py:445
  40.0 1.0 %copy.8 = bf16[1,128,4096]{2,1,0:T(8,128)(2,1)} copy(bf16[1,128,4096]{2,1,0:T(8,128)(2,1)S(1)} %bitcast.6) | data formatting | bytes 2097152

commit v2 on v1

v2 whole, which is shorter than its diff:
```python
import functools

import jax
import jax.numpy as jnp
import numpy as np
from jax import lax
from jax.experimental import pallas as pl
from jax.experimental.pallas import tpu as pltpu
from jax.sharding import PartitionSpec as P

CACHE = 256
MESH = pl.DeviceIdType.MESH


def attention_kernel(
    n,
    sections,
    docs_hbm,
    signs_hbm,
    q_hbm,
    k_hbm,
    v_hbm,
    cache_hbm,
    out_ref,
    docs_ref,
    signs_ref,
    q_buf,
    q_send,
    cache_buf,
    own,
    held,
    out_buf,
    small_sem,
    cache_sem,
    q_sem,
    swap_send,
    swap_recv,
    own_sem,
    mine_sem,
    send_sem,
    recv_sem,
    out_send,
    out_recv,
):
    section = lax.axis_index("section")
    me = lax.axis_index("ctx")
    p = lax.rem(me, 2)
    chip = me // 2
    chips = n // 2
    heads, hd = held.shape[0], held.shape[4]
    rows = held.shape[3]
    slots = held.shape[2]
    back = (slots - 2) // 2
    width = out_buf.shape[3]
    groups = width // hd
    all_heads = 2 * heads
    kv_width = all_heads * hd
    detour = chips == 4
    sibling = me + 1 - 2 * p
    following = lax.rem(section + 1, sections)
    previous = lax.rem(section + sections - 1, sections)

    def cols(start, size):
        return pl.ds(pl.multiple_of(start, hd), size)

    barrier = pltpu.get_barrier_semaphore()

    def greet(sec, ctx):
        pl.semaphore_signal(barrier, inc=1, device_id=(sec, ctx), device_id_type=MESH)

    own_copies = (
        pltpu.make_async_copy(k_hbm, own.at[0], own_sem),
        pltpu.make_async_copy(v_hbm, own.at[1], own_sem),
    )

    def mine_copies(i):
        at = cols((p * heads + i) * hd, hd)
        slot = slots - 2 + p
        return (
            pltpu.make_async_copy(k_hbm.at[:, at], held.at[i, 0, slot], mine_sem),
            pltpu.make_async_copy(v_hbm.at[:, at], held.at[i, 1, slot], mine_sem),
        )

    span = heads * width
    q_copies = (
        pltpu.make_async_copy(q_hbm.at[:, cols(p * span, span)], q_buf.at[p], q_sem.at[0]),
        pltpu.make_async_copy(q_hbm.at[:, cols((1 - p) * span, span)], q_send, q_sem.at[1]),
    )
    reach = heads * hd
    cache_copies = (
        pltpu.make_async_copy(
            cache_hbm.at[:, cols(p * reach, reach)], cache_buf.at[0], cache_sem
        ),
        pltpu.make_async_copy(
            cache_hbm.at[:, cols(kv_width + p * reach, reach)], cache_buf.at[1], cache_sem
        ),
    )
    small = (
        pltpu.make_async_copy(docs_hbm, docs_ref, small_sem.at[0]),
        pltpu.make_async_copy(signs_hbm, signs_ref, small_sem.at[1]),
    )
    def all_of(ref, sem):
        return pltpu.make_async_remote_copy(
            src_ref=ref,
            dst_ref=ref,
            send_sem=sem,
            recv_sem=sem,
            device_id=(section, sibling),
            device_id_type=MESH,
        )

    for copy in own_copies:
        copy.start()

    for d in range(back, 0, -1):
        come = chip >= d
        if detour and d == 1:
            come = come & ((chip != 2) | (p == 0))

        @pl.when(come)
        def _(d=d):
            greet(section, 2 * (chip - d))
            greet(section, 2 * (chip - d) + 1)
    if detour:
        @pl.when(chip == 2)
        def _():
            greet(section, me + 2)
    greet(section, sibling)
    greet(previous, 2 * chip)
    greet(previous, 2 * chip + 1)

    for copy in small + mine_copies(0) + cache_copies + q_copies:
        copy.start()
    for i in range(1, heads):
        for copy in mine_copies(i):
            copy.start()

    for d in range(1, back + 1):
        @pl.when(chip < d)
        def _(d=d):
            for i in range(heads):
                at = slots - 2 - 2 * d
                held[i, :, at : at + 2] = jnp.zeros((2, 2, rows, hd), held.dtype)

    low = lax.broadcasted_iota(jnp.int32, (hd, hd), 0) & lax.broadcasted_iota(
        jnp.int32, (hd, hd), 1
    )
    shift = 1
    while 2 * shift < hd:
        shift *= 2
    while shift:
        low = low ^ (low >> shift)
        shift //= 2
    hada = (1 - 2 * (low & 1)).astype(jnp.float32).astype(jnp.bfloat16)

    count = jnp.int32(3)
    for d in range(1, back + 1):
        count = count + jnp.where(chip + d < chips, 2, 0)
    if detour:
        count = count + jnp.where(chip == chips - 1, 1, 0) - jnp.where(chip == 1, 1, 0)
    pl.semaphore_wait(barrier, count)

    def remote(src, dst, index, i, pair, target):
        return pltpu.make_async_remote_copy(
            src_ref=src,
            dst_ref=dst,
            send_sem=send_sem.at[index],
            recv_sem=recv_sem.at[i, pair],
            device_id=(section, target),
            device_id_type=MESH,
        )

    swap_q = pltpu.make_async_remote_copy(
        src_ref=q_send,
        dst_ref=q_buf.at[p],
        send_sem=swap_send,
        recv_sem=swap_recv,
        device_id=(section, sibling),
        device_id_type=MESH,
    )

    def piece(h):
        return own.at[:, :, cols(h * hd, hd)]

    def swap_kv(i):
        block = piece((1 - p) * heads + i)
        return remote(block, held.at[i, :, slots - 2 + p], 0, i, back, sibling)

    def ahead(i):
        for core in range(2):
            for d in range(1, back + 1):
                go = chip + d < chips
                if detour and d == 1:
                    go = go & ((chip != 1) | (i == 0)) if core == 0 else go & (chip != 1)

                @pl.when(go)
                def _(core=core, d=d):
                    slot = slots - 2 - 2 * d + p
                    block = piece(core * heads + i)
                    target = 2 * (chip + d) + core
                    remote(
                        block, held.at[i, :, slot], 2 * d - 1 + core, i, back - d, target
                    ).start()

    def relay_copy(i):
        return remote(held.at[i, :, 0:2], held.at[i, :, 2:4], 1, i, 1, me - 2)

    def arrived(i, pair):
        block = held.at[i, :, 2 * pair : 2 * pair + 2]
        remote(block, block, 0, i, pair, sibling).wait_recv()

    relays = (chip == chips - 1) if detour else False

    def relay(i):
        if detour:
            @pl.when(relays)
            def _():
                arrived(i, 0)

                @pl.when((i > 0) | (p == 1))
                def _():
                    relay_copy(i).start()

    def send(i, carry):
        swap_kv(i).start()
        ahead(i)
        return carry

    all_of(own, own_sem).wait_recv()
    lax.fori_loop(0, heads, send, 0)
    q_copies[1].wait()
    swap_q.start()

    for copy in small:
        copy.wait()
    root = hd ** -0.5
    sign_k = signs_ref[0:1, :].astype(jnp.float32) * root
    sign_v = signs_ref[1:2, :].astype(jnp.float32) * root
    factor = root * float(np.log2(np.e))
    causal = lax.broadcasted_iota(jnp.int32, (rows, rows), 1) <= lax.broadcasted_iota(
        jnp.int32, (rows, rows), 0
    )

    def out_copy(i, e):
        return pltpu.make_async_remote_copy(
            src_ref=out_buf.at[i, e],
            dst_ref=out_ref.at[:, cols((p * heads + i) * width, width)],
            send_sem=out_send,
            recv_sem=out_recv,
            device_id=(following, 2 * chip + e),
            device_id_type=MESH,
        )

    def first_copy(g):
        return pltpu.make_async_remote_copy(
            src_ref=out_buf.at[0, p, :, g * hd : (g + 1) * hd],
            dst_ref=out_ref.at[:, cols(p * heads * width + g * hd, hd)],
            send_sem=out_send,
            recv_sem=out_recv,
            device_id=(following, me),
            device_id_type=MESH,
        )

    def step(t, carry):
        i = t // 2
        half = lax.rem(t, 2)
        e = (p + half) - 2 * p * half

        @pl.when(t == 0)
        def _():
            all_of(cache_buf, cache_sem).wait_recv()
            all_of(held.at[:, :, slots - 2 + p], mine_sem).wait_recv()
            q_copies[0].wait()

        stretch = 2 * chip + e
        doc = docs_ref[stretch]
        picks = [
            jnp.full((1, hd), jnp.where(doc == k, 1.0, 0.0), jnp.float32).astype(jnp.bfloat16)
            for k in range(cache_buf.shape[1] // CACHE)
        ]

        def cache_block(kind):
            terms = [
                cache_buf[kind, k * CACHE : (k + 1) * CACHE, cols(i * hd, hd)] * pick
                for k, pick in enumerate(picks)
            ]
            return functools.reduce(jnp.add, terms)

        back_k = jnp.dot(cache_block(0), hada, preferred_element_type=jnp.float32)
        back_v = jnp.dot(cache_block(1), hada, preferred_element_type=jnp.float32)
        back_k = (back_k * sign_k).astype(jnp.bfloat16)
        back_v = (back_v * sign_v).astype(jnp.bfloat16)
        biases = []
        for d in range(slots - 2, 0, -1):
            seen = (stretch >= d) & (docs_ref[jnp.maximum(stretch - d, 0)] == doc)
            biases.append(jnp.where(seen, 0.0, -jnp.inf).astype(jnp.float32))

        @pl.when(half == 0)
        def _():
            for pair in range(back):
                there = chip - back + pair >= 0
                if detour and pair == 0:
                    there = there & (chip != chips - 1)

                @pl.when(there)
                def _(pair=pair):
                    arrived(i, pair)

        @pl.when(half == 1 - p)
        def _():
            block = held.at[i, :, slots - 1 - p]
            remote(block, block, 0, i, back, sibling).wait_recv()

        @pl.when(t == 1)
        def _():
            swap_q.wait_recv()

        span_new = (slots - 1) * rows
        keys = held[i, 0, pl.ds(e, slots - 1)].reshape(span_new, hd)
        values = held[i, 1, pl.ds(e, slots - 1)].reshape(span_new, hd)
        keys = jnp.concatenate([back_k, keys], axis=0)
        values = jnp.concatenate([back_v, values], axis=0)
        for g in range(groups):
            query = q_buf[e, :, cols(i * width + g * hd, hd)]
            scores = lax.dot_general(
                query, keys, (((1,), (1,)), ((), ())), preferred_element_type=jnp.float32
            )
            parts = [scores[:, at : at + rows] for at in range(0, CACHE, rows)]
            for d in range(slots - 2):
                at = CACHE + rows * d
                parts.append(scores[:, at : at + rows] + biases[d])
            parts.append(jnp.where(causal, scores[:, CACHE + span_new - rows :], -jnp.inf))
            top = functools.reduce(jnp.maximum, parts)
            top = jnp.max(top, axis=1, keepdims=True)
            expo = [jnp.exp2((part - top) * factor) for part in parts]
            total = jnp.sum(functools.reduce(jnp.add, expo), axis=1, keepdims=True)
            weights = jnp.concatenate([part.astype(jnp.bfloat16) for part in expo], axis=1)
            summed = jnp.dot(weights, values, preferred_element_type=jnp.float32)
            out_buf[i, e, :, g * hd : (g + 1) * hd] = (summed / total).astype(out_buf.dtype)

            @pl.when(t == 0)
            def _(g=g):
                first_copy(g).start()

        @pl.when(t > 0)
        def _():
            out_copy(i, e).start()

        @pl.when((half == 0) & (i + 1 < heads))
        def _():
            relay(i + 1)

        return carry

    relay(0)
    lax.fori_loop(0, 2 * heads, step, 0)

    def leaving(core):
        return own.at[:, :, cols(core * heads * hd, heads * hd)]

    all_of(leaving(1 - p), send_sem.at[0]).wait_send()
    swap_q.wait_send()
    for core in range(2):
        for d in range(1, back + 1):
            go = chip + d < chips
            if detour and d == 1:
                go = go & (chip != 1)

            @pl.when(go)
            def _(core=core, d=d):
                all_of(leaving(core), send_sem.at[2 * d - 1 + core]).wait_send()
    if detour:
        @pl.when(chip == 1)
        def _():
            all_of(piece(0), send_sem.at[1]).wait_send()

        @pl.when(relays & (p == 0))
        def _():
            all_of(held.at[1:, :, 0:2], send_sem.at[1]).wait_send()

        @pl.when(relays & (p == 1))
        def _():
            all_of(held.at[:, :, 0:2], send_sem.at[1]).wait_send()
    all_of(out_buf, out_send).wait_send()
    all_of(out_ref, out_recv).wait_recv()


def per_device(n, sections, queries, keys_new, values_new, stretch_cache, signs, docs):
    rows, q_width = queries.shape[1:]
    kv_width = keys_new.shape[-1]
    hd = signs.shape[-1]
    all_heads = kv_width // hd
    heads = all_heads // 2
    width = q_width // all_heads
    groups = width // hd
    reach = n // 2
    slots = reach + 2
    cached = stretch_cache.shape[1]
    dtype = queries.dtype
    dma = pltpu.SemaphoreType.DMA
    in_hbm = pl.BlockSpec(memory_space=pltpu.HBM)
    out = pl.pallas_call(
        functools.partial(attention_kernel, n, sections),
        out_shape=pltpu.VMEM((rows, q_width), dtype),
        in_specs=[in_hbm] * 6,
        out_specs=pl.BlockSpec(memory_space=pltpu.VMEM),
        scratch_shapes=[
            pltpu.SMEM(docs.shape, docs.dtype),
            pltpu.VMEM(signs.shape[1:], signs.dtype),
            pltpu.VMEM((2, rows, heads * width), dtype),
            pltpu.VMEM((rows, heads * width), dtype),
            pltpu.VMEM((2, cached, heads * hd), dtype),
            pltpu.VMEM((2, rows, kv_width), dtype),
            pltpu.VMEM((heads, 2, slots, rows, hd), dtype),
            pltpu.VMEM((heads, 2, rows, width), dtype),
            dma((2,)),
            dma,
            dma((2,)),
            dma,
            dma,
            dma,
            dma,
            dma((reach + 1,)),
            dma((heads, reach // 2 + 1)),
            dma,
            dma,
        ],
        compiler_params=pltpu.CompilerParams(
            collective_id=0, has_side_effects=True, vmem_limit_bytes=58 * 1024 * 1024
        ),
    )(docs, signs[0], queries[0], keys_new[0], values_new[0], stretch_cache[0])
    return out[None]


def solution(mesh):
    in_specs = (
        P("section", "ctx", None),
        P("section", "ctx", None),
        P("section", "ctx", None),
        P("section", None, None),
        P("section", None, None),
        P(),
    )
    out_specs = P("section", "ctx", None)
    body = functools.partial(per_device, mesh.shape["ctx"], mesh.shape["section"])
    return jax.shard_map(body, mesh=mesh, in_specs=in_specs, out_specs=out_specs, check_vma=False)
```

time: 41.4 us -> 38.7 us (0.935)
  Pallas kernels: 39.9 us -> 37.6 us
    pallas_call x1, Pallas kernels: 39.9 us -> 37.6 us  [per_device(): pl.pallas_call(functools.partial(attention_kernel, n, sections), out_shap...]
where the time goes in v2:
time: 38.7 us; the launch traced here: 38.6 us
  Pallas kernels  37.6 us (97%)
  local copies, waits for them, and re-layouts  0.97 us (3%)
    pallas_call x1, Pallas kernels, per_device(): pl.pallas_call(functools.partial(attention_kernel, n, sections), out_shap...  37.6 us
    unnamed x1, local copies, waits for them, and re-layouts  0.97 us

profile of v2, /device:TPU:4, one launch (start us, length us, event | category | flops | bytes accessed | tf_op | source)
XLA Modules:
  0.0 38.6 jit_solution(7115878118059551940)
XLA Ops:
  0.0 37.6 %shard_map.64 = bf16[128,4096]{1,0:T(8,128)(2,1)S(1)} custom-call(s32[8]{0:T(128)} %docs_hbm.1, s32[2,128]{1,0:T(2,128)} %bitcast.11, bf16[128,4096]{1,0:T(8,128)(2,1)} %bitcast.8, bf16[128,1024]{1,0:T(8,128)(2,1)} %bitcast.9, bf16[128,1024]{1,0:T(8,128)(2,1)} %bitcast.10, bf16[512,2048]{1,0:T(8,128)(2,1)} %bitcast.7), custom_call_target="tpu_custom_call" | custom-call | tf_op jit(solution)/shard_map/pallas_call | solution.py:402
  37.6 1.0 %copy.8 = bf16[1,128,4096]{2,1,0:T(8,128)(2,1)} copy(bf16[1,128,4096]{2,1,0:T(8,128)(2,1)S(1)} %bitcast.6) | data formatting | bytes 2097152

commit v3 on v2

--- a/solution.py
+++ b/solution.py
@@ -9,6 +9,7 @@
 from jax.sharding import PartitionSpec as P
 
 CACHE = 256
+LENT = (3, 7)
 MESH = pl.DeviceIdType.MESH
 
 
@@ -41,6 +42,8 @@
     recv_sem,
     out_send,
     out_recv,
+    pass_buf,
+    pass_sem,
 ):
     section = lax.axis_index("section")
     me = lax.axis_index("ctx")
@@ -125,6 +128,10 @@
         @pl.when(chip == 2)
         def _():
             greet(section, me + 2)
+
+        @pl.when(chip == 0)
+        def _():
+            greet(section, me + 4)
     greet(section, sibling)
     greet(previous, 2 * chip)
     greet(previous, 2 * chip + 1)
@@ -157,7 +164,7 @@
     for d in range(1, back + 1):
         count = count + jnp.where(chip + d < chips, 2, 0)
     if detour:
-        count = count + jnp.where(chip == chips - 1, 1, 0) - jnp.where(chip == 1, 1, 0)
+        count = count + jnp.where(chip >= 2, 1, 0) - jnp.where(chip == 1, 1, 0)
     pl.semaphore_wait(barrier, count)
 
     def remote(src, dst, index, i, pair, target):
@@ -260,6 +267,35 @@
             device_id=(following, me),
             device_id_type=MESH,
         )
+
+    def hop(src, dst, sem, recv, target):
+        return pltpu.make_async_remote_copy(
+            src_ref=src,
+            dst_ref=dst,
+            send_sem=sem,
+            recv_sem=recv,
+            device_id=target,
+            device_id_type=MESH,
+        )
+
+    lent, held_back = LENT
+    lender = (chip == 2) if detour else False
+    lent_half = lent % 2
+    lent_e = (p + lent_half) - 2 * p * lent_half
+    lent_out = out_ref.at[:, cols((p * heads + lent // 2) * width, width)]
+
+    def lend():
+        return hop(
+            out_buf.at[lent // 2, lent_e], pass_buf.at[0], out_send, pass_sem.at[0], (section, p)
+        )
+
+    def carry_on():
+        return hop(
+            pass_buf.at[0], pass_buf.at[1], pass_sem.at[1], pass_sem.at[2], (following, me)
+        )
+
+    def hand_over():
+        return hop(pass_buf.at[1], lent_out, pass_sem.at[3], out_recv, (section, 4 + lent_e))
 
     def step(t, carry):
         i = t // 2
@@ -342,7 +378,17 @@
             def _(g=g):
                 first_copy(g).start()
 
-        @pl.when(t > 0)
+        if detour:
+            @pl.when((chip == 0) & (t == held_back))
+            def _():
+                lend().wait_recv()
+                carry_on().start()
+
+            @pl.when(lender & (t == lent))
+            def _():
+                lend().start()
+
+        @pl.when((t > 0) & jnp.logical_not(lender & (t == lent)))
         def _():
             out_copy(i, e).start()
 
@@ -354,6 +400,12 @@
 
     relay(0)
     lax.fori_loop(0, 2 * heads, step, 0)
+
+    if detour:
+        @pl.when(chip == 0)
+        def _():
+            carry_on().wait_recv()
+            hand_over().start()
 
     def leaving(core):
         return own.at[:, :, cols(core * heads * hd, heads * hd)]
@@ -381,6 +433,12 @@
         @pl.when(relays & (p == 1))
         def _():
             all_of(held.at[:, :, 0:2], send_sem.at[1]).wait_send()
+    if detour:
+        @pl.when(chip == 0)
+        def _():
+            carry_on().wait_send()
+            hand_over().wait_send()
+
     all_of(out_buf, out_send).wait_send()
     all_of(out_ref, out_recv).wait_recv()
 
@@ -424,6 +482,8 @@
             dma((heads, reach // 2 + 1)),
             dma,
             dma,
+            pltpu.VMEM((2, rows, width), dtype),
+            dma((4,)),
         ],
         compiler_params=pltpu.CompilerParams(
             collective_id=0, has_side_effects=True, vmem_limit_bytes=58 * 1024 * 1024

time: 38.7 us -> 37.3 us (0.964)
  Pallas kernels: 37.6 us -> 36 us
    pallas_call x1, Pallas kernels: 37.6 us -> 36 us  [per_device(): pl.pallas_call(functools.partial(attention_kernel, n, sections), out_shap...]
where the time goes in v3:
time: 37.3 us; the launch traced here: 37 us
  Pallas kernels  36 us (97%)
  local copies, waits for them, and re-layouts  0.97 us (3%)
    pallas_call x1, Pallas kernels, per_device(): pl.pallas_call(functools.partial(attention_kernel, n, sections), out_shap...  36 us
    unnamed x1, local copies, waits for them, and re-layouts  0.97 us

profile of v3, /device:TPU:4, one launch (start us, length us, event | category | flops | bytes accessed | tf_op | source)
XLA Modules:
  0.0 37.0 jit_solution(1421882249887221412)
XLA Ops:
  0.0 36.0 %shard_map.64 = bf16[128,4096]{1,0:T(8,128)(2,1)S(1)} custom-call(s32[8]{0:T(128)} %docs_hbm.1, s32[2,128]{1,0:T(2,128)} %bitcast.11, bf16[128,4096]{1,0:T(8,128)(2,1)} %bitcast.8, bf16[128,1024]{1,0:T(8,128)(2,1)} %bitcast.9, bf16[128,1024]{1,0:T(8,128)(2,1)} %bitcast.10, bf16[512,2048]{1,0:T(8,128)(2,1)} %bitcast.7), custom_call_target="tpu_custom_call" | custom-call | tf_op jit(solution)/shard_map/pallas_call | solution.py:460
  36.1 1.0 %copy.8 = bf16[1,128,4096]{2,1,0:T(8,128)(2,1)} copy(bf16[1,128,4096]{2,1,0:T(8,128)(2,1)S(1)} %bitcast.6) | data formatting | bytes 2097152

commit v4 on v3

--- a/solution.py
+++ b/solution.py
@@ -9,7 +9,8 @@
 from jax.sharding import PartitionSpec as P
 
 CACHE = 256
-LENT = (3, 7)
+LENT = (4, 7)
+PARTS = 3
 MESH = pl.DeviceIdType.MESH
 
 
@@ -117,9 +118,6 @@
 
     for d in range(back, 0, -1):
         come = chip >= d
-        if detour and d == 1:
-            come = come & ((chip != 2) | (p == 0))
-
         @pl.when(come)
         def _(d=d):
             greet(section, 2 * (chip - d))
@@ -164,7 +162,7 @@
     for d in range(1, back + 1):
         count = count + jnp.where(chip + d < chips, 2, 0)
     if detour:
-        count = count + jnp.where(chip >= 2, 1, 0) - jnp.where(chip == 1, 1, 0)
+        count = count + jnp.where(chip >= 2, 1, 0)
     pl.semaphore_wait(barrier, count)
 
     def remote(src, dst, index, i, pair, target):
@@ -198,7 +196,7 @@
             for d in range(1, back + 1):
                 go = chip + d < chips
                 if detour and d == 1:
-                    go = go & ((chip != 1) | (i == 0)) if core == 0 else go & (chip != 1)
+                    go = go & ((chip != 1) | (i == 0))
 
                 @pl.when(go)
                 def _(core=core, d=d):
@@ -224,7 +222,7 @@
             def _():
                 arrived(i, 0)
 
-                @pl.when((i > 0) | (p == 1))
+                @pl.when(i > 0)
                 def _():
                     relay_copy(i).start()
 
@@ -248,23 +246,13 @@
         jnp.int32, (rows, rows), 0
     )
 
-    def out_copy(i, e):
+    def out_copy(i, e, start, size):
         return pltpu.make_async_remote_copy(
-            src_ref=out_buf.at[i, e],
-            dst_ref=out_ref.at[:, cols((p * heads + i) * width, width)],
+            src_ref=out_buf.at[i, e, :, start : start + size],
+            dst_ref=out_ref.at[:, cols((p * heads + i) * width + start, size)],
             send_sem=out_send,
             recv_sem=out_recv,
             device_id=(following, 2 * chip + e),
-            device_id_type=MESH,
-        )
-
-    def first_copy(g):
-        return pltpu.make_async_remote_copy(
-            src_ref=out_buf.at[0, p, :, g * hd : (g + 1) * hd],
-            dst_ref=out_ref.at[:, cols(p * heads * width + g * hd, hd)],
-            send_sem=out_send,
-            recv_sem=out_recv,
-            device_id=(following, me),
             device_id_type=MESH,
         )
 
@@ -282,11 +270,17 @@
     lender = (chip == 2) if detour else False
     lent_half = lent % 2
     lent_e = (p + lent_half) - 2 * p * lent_half
-    lent_out = out_ref.at[:, cols((p * heads + lent // 2) * width, width)]
+    share = pass_buf.shape[2]
+    kept = width - share
+    lent_out = out_ref.at[:, cols((p * heads + lent // 2) * width + kept, share)]
 
     def lend():
         return hop(
-            out_buf.at[lent // 2, lent_e], pass_buf.at[0], out_send, pass_sem.at[0], (section, p)
+            out_buf.at[lent // 2, lent_e, :, kept:],
+            pass_buf.at[0],
+            out_send,
+            pass_sem.at[0],
+            (section, p),
         )
 
     def carry_on():
@@ -301,6 +295,8 @@
         i = t // 2
         half = lax.rem(t, 2)
         e = (p + half) - 2 * p * half
+        lends = lender & (t == lent)
+        in_parts = (t > 0) & ((t < PARTS) | lends)
 
         @pl.when(t == 0)
         def _():
@@ -376,7 +372,12 @@
 
             @pl.when(t == 0)
             def _(g=g):
-                first_copy(g).start()
+                out_copy(i, e, g * hd, hd).start()
+
+            if g == groups // 2 - 1:
+                @pl.when(in_parts)
+                def _():
+                    out_copy(i, e, 0, width // 2).start()
 
         if detour:
             @pl.when((chip == 0) & (t == held_back))
@@ -384,13 +385,17 @@
                 lend().wait_recv()
                 carry_on().start()
 
-            @pl.when(lender & (t == lent))
+            @pl.when(lends)
             def _():
                 lend().start()
 
-        @pl.when((t > 0) & jnp.logical_not(lender & (t == lent)))
-        def _():
-            out_copy(i, e).start()
+        @pl.when(in_parts & jnp.logical_not(lends))
+        def _():
+            out_copy(i, e, width // 2, width // 2).start()
+
+        @pl.when((t >= PARTS) & jnp.logical_not(lends))
+        def _():
+            out_copy(i, e, 0, width).start()
 
         @pl.when((half == 0) & (i + 1 < heads))
         def _():
@@ -424,15 +429,12 @@
     if detour:
         @pl.when(chip == 1)
         def _():
-            all_of(piece(0), send_sem.at[1]).wait_send()
-
-        @pl.when(relays & (p == 0))
+            for core in range(2):
+                all_of(piece(0), send_sem.at[1 + core]).wait_send()
+
+        @pl.when(relays)
         def _():
             all_of(held.at[1:, :, 0:2], send_sem.at[1]).wait_send()
-
-        @pl.when(relays & (p == 1))
-        def _():
-            all_of(held.at[:, :, 0:2], send_sem.at[1]).wait_send()
     if detour:
         @pl.when(chip == 0)
         def _():
@@ -482,7 +484,7 @@
             dma((heads, reach // 2 + 1)),
             dma,
             dma,
-            pltpu.VMEM((2, rows, width), dtype),
+            pltpu.VMEM((2, rows, width // 2), dtype),
             dma((4,)),
         ],
         compiler_params=pltpu.CompilerParams(

time: 37.3 us -> 36.6 us (0.981)
  Pallas kernels: 36 us -> 35.5 us
    pallas_call x1, Pallas kernels: 36 us -> 35.5 us  [per_device(): pl.pallas_call(functools.partial(attention_kernel, n, sections), out_shap...]
where the time goes in v4:
time: 36.6 us; the launch traced here: 36.5 us
  Pallas kernels  35.5 us (97%)
  local copies, waits for them, and re-layouts  0.97 us (3%)
    pallas_call x1, Pallas kernels, per_device(): pl.pallas_call(functools.partial(attention_kernel, n, sections), out_shap...  35.5 us
    unnamed x1, local copies, waits for them, and re-layouts  0.97 us

profile of v4, /device:TPU:4, one launch (start us, length us, event | category | flops | bytes accessed | tf_op | source)
XLA Modules:
  0.0 36.5 jit_solution(2248402745273198364)
XLA Ops:
  0.0 35.5 %shard_map.64 = bf16[128,4096]{1,0:T(8,128)(2,1)S(1)} custom-call(s32[8]{0:T(128)} %docs_hbm.1, s32[2,128]{1,0:T(2,128)} %bitcast.11, bf16[128,4096]{1,0:T(8,128)(2,1)} %bitcast.8, bf16[128,1024]{1,0:T(8,128)(2,1)} %bitcast.9, bf16[128,1024]{1,0:T(8,128)(2,1)} %bitcast.10, bf16[512,2048]{1,0:T(8,128)(2,1)} %bitcast.7), custom_call_target="tpu_custom_call" | custom-call | tf_op jit(solution)/shard_map/pallas_call | solution.py:462
  35.5 1.0 %copy.8 = bf16[1,128,4096]{2,1,0:T(8,128)(2,1)} copy(bf16[1,128,4096]{2,1,0:T(8,128)(2,1)S(1)} %bitcast.6) | data formatting | bytes 2097152

commit v5 on v4

--- a/solution.py
+++ b/solution.py
@@ -191,21 +191,20 @@
         block = piece((1 - p) * heads + i)
         return remote(block, held.at[i, :, slots - 2 + p], 0, i, back, sibling)
 
-    def ahead(i):
-        for core in range(2):
-            for d in range(1, back + 1):
-                go = chip + d < chips
-                if detour and d == 1:
-                    go = go & ((chip != 1) | (i == 0))
-
-                @pl.when(go)
-                def _(core=core, d=d):
-                    slot = slots - 2 - 2 * d + p
-                    block = piece(core * heads + i)
-                    target = 2 * (chip + d) + core
-                    remote(
-                        block, held.at[i, :, slot], 2 * d - 1 + core, i, back - d, target
-                    ).start()
+    def ahead(i, core):
+        for d in range(1, back + 1):
+            go = chip + d < chips
+            if detour and d == 1:
+                go = go & ((chip != 1) | (i == 0))
+
+            @pl.when(go)
+            def _(d=d):
+                slot = slots - 2 - 2 * d + p
+                block = piece(core * heads + i)
+                target = 2 * (chip + d) + core
+                remote(
+                    block, held.at[i, :, slot], 2 * d - 1 + core, i, back - d, target
+                ).start()
 
     def relay_copy(i):
         return remote(held.at[i, :, 0:2], held.at[i, :, 2:4], 1, i, 1, me - 2)
@@ -226,13 +225,22 @@
                 def _():
                     relay_copy(i).start()
 
-    def send(i, carry):
-        swap_kv(i).start()
-        ahead(i)
+    def send(k, carry):
+        i, core = k // 2, lax.rem(k, 2)
+        if detour and heads % 2 == 0:
+            pairs = chip == 1
+            i = jnp.where(pairs, 2 * (k // 4) + lax.rem(k, 2), i)
+            core = jnp.where(pairs, lax.rem(k // 2, 2), core)
+
+        @pl.when(core == 0)
+        def _():
+            swap_kv(i).start()
+
+        ahead(i, core)
         return carry
 
     all_of(own, own_sem).wait_recv()
-    lax.fori_loop(0, heads, send, 0)
+    lax.fori_loop(0, 2 * heads, send, 0)
     q_copies[1].wait()
     swap_q.start()
 

time: 36.6 us -> 36.2 us (0.989)
  Pallas kernels: 35.5 us -> 35.1 us
    pallas_call x1, Pallas kernels: 35.5 us -> 35.1 us  [per_device(): pl.pallas_call(functools.partial(attention_kernel, n, sections), out_shap...]
where the time goes in v5:
time: 36.2 us; the launch traced here: 36 us
  Pallas kernels  35.1 us (97%)
  local copies, waits for them, and re-layouts  0.97 us (3%)
    pallas_call x1, Pallas kernels, per_device(): pl.pallas_call(functools.partial(attention_kernel, n, sections), out_shap...  35.1 us
    unnamed x1, local copies, waits for them, and re-layouts  0.97 us

profile of v5, /device:TPU:4, one launch (start us, length us, event | category | flops | bytes accessed | tf_op | source)
XLA Modules:
  0.0 36.0 jit_solution(7191818021991600435)
XLA Ops:
  0.0 35.1 %shard_map.64 = bf16[128,4096]{1,0:T(8,128)(2,1)S(1)} custom-call(s32[8]{0:T(128)} %docs_hbm.1, s32[2,128]{1,0:T(2,128)} %bitcast.11, bf16[128,4096]{1,0:T(8,128)(2,1)} %bitcast.8, bf16[128,1024]{1,0:T(8,128)(2,1)} %bitcast.9, bf16[128,1024]{1,0:T(8,128)(2,1)} %bitcast.10, bf16[512,2048]{1,0:T(8,128)(2,1)} %bitcast.7), custom_call_target="tpu_custom_call" | custom-call | tf_op jit(solution)/shard_map/pallas_call | solution.py:470
  35.1 1.0 %copy.8 = bf16[1,128,4096]{2,1,0:T(8,128)(2,1)} copy(bf16[1,128,4096]{2,1,0:T(8,128)(2,1)S(1)} %bitcast.6) | data formatting | bytes 2097152

commit v6 on v5

--- a/solution.py
+++ b/solution.py
@@ -304,7 +304,7 @@
         half = lax.rem(t, 2)
         e = (p + half) - 2 * p * half
         lends = lender & (t == lent)
-        in_parts = (t > 0) & ((t < PARTS) | lends)
+        in_parts = (t == 1) | lends
 
         @pl.when(t == 0)
         def _():
@@ -378,9 +378,14 @@
             summed = jnp.dot(weights, values, preferred_element_type=jnp.float32)
             out_buf[i, e, :, g * hd : (g + 1) * hd] = (summed / total).astype(out_buf.dtype)
 
-            @pl.when(t == 0)
+            @pl.when((t == 0) | (t == 2))
             def _(g=g):
                 out_copy(i, e, g * hd, hd).start()
+
+            if g == groups // 2:
+                @pl.when((half == 0) & (i + 1 < heads))
+                def _():
+                    relay(i + 1)
 
             if g == groups // 2 - 1:
                 @pl.when(in_parts)
@@ -404,10 +409,6 @@
         @pl.when((t >= PARTS) & jnp.logical_not(lends))
         def _():
             out_copy(i, e, 0, width).start()
-
-        @pl.when((half == 0) & (i + 1 < heads))
-        def _():
-            relay(i + 1)
 
         return carry
 

time: 36.2 us -> 36.2 us (level)
  no operation moved by 1% of the time
where the time goes in v6:
time: 36.2 us; the launch traced here: 36.1 us
  Pallas kernels  35.1 us (97%)
  local copies, waits for them, and re-layouts  0.97 us (3%)
    pallas_call x1, Pallas kernels, per_device(): pl.pallas_call(functools.partial(attention_kernel, n, sections), out_shap...  35.1 us
    unnamed x1, local copies, waits for them, and re-layouts  0.97 us

profile of v6, /device:TPU:4, one launch (start us, length us, event | category | flops | bytes accessed | tf_op | source)
XLA Modules:
  0.0 36.1 jit_solution(15086458892512332464)
XLA Ops:
  0.0 35.1 %shard_map.64 = bf16[128,4096]{1,0:T(8,128)(2,1)S(1)} custom-call(s32[8]{0:T(128)} %docs_hbm.1, s32[2,128]{1,0:T(2,128)} %bitcast.11, bf16[128,4096]{1,0:T(8,128)(2,1)} %bitcast.8, bf16[128,1024]{1,0:T(8,128)(2,1)} %bitcast.9, bf16[128,1024]{1,0:T(8,128)(2,1)} %bitcast.10, bf16[512,2048]{1,0:T(8,128)(2,1)} %bitcast.7), custom_call_target="tpu_custom_call" | custom-call | tf_op jit(solution)/shard_map/pallas_call | solution.py:471
  35.1 1.0 %copy.8 = bf16[1,128,4096]{2,1,0:T(8,128)(2,1)} copy(bf16[1,128,4096]{2,1,0:T(8,128)(2,1)S(1)} %bitcast.6) | data formatting | bytes 2097152

commit v7 on v6

--- a/solution.py
+++ b/solution.py
@@ -304,7 +304,7 @@
         half = lax.rem(t, 2)
         e = (p + half) - 2 * p * half
         lends = lender & (t == lent)
-        in_parts = (t == 1) | lends
+        in_parts = t == 1
 
         @pl.when(t == 0)
         def _():
@@ -387,6 +387,11 @@
                 def _():
                     relay(i + 1)
 
+            if g == kept // hd - 1:
+                @pl.when(lends)
+                def _():
+                    out_copy(i, e, 0, kept).start()
+
             if g == groups // 2 - 1:
                 @pl.when(in_parts)
                 def _():
@@ -402,7 +407,7 @@
             def _():
                 lend().start()
 
-        @pl.when(in_parts & jnp.logical_not(lends))
+        @pl.when(in_parts)
         def _():
             out_copy(i, e, width // 2, width // 2).start()
 
@@ -493,7 +498,7 @@
             dma((heads, reach // 2 + 1)),
             dma,
             dma,
-            pltpu.VMEM((2, rows, width // 2), dtype),
+            pltpu.VMEM((2, rows, width // 4 * 3), dtype),
             dma((4,)),
         ],
         compiler_params=pltpu.CompilerParams(

time: 36.2 us -> 36.2 us (level)
  no operation moved by 1% of the time
where the time goes in v7:
time: 36.2 us; the launch traced here: 36.1 us
  Pallas kernels  35.1 us (97%)
  local copies, waits for them, and re-layouts  0.97 us (3%)
    pallas_call x1, Pallas kernels, per_device(): pl.pallas_call(functools.partial(attention_kernel, n, sections), out_shap...  35.1 us
    unnamed x1, local copies, waits for them, and re-layouts  0.97 us

profile of v7, /device:TPU:4, one launch (start us, length us, event | category | flops | bytes accessed | tf_op | source)
XLA Modules:
  0.0 36.1 jit_solution(425339776268125836)
XLA Ops:
  0.0 35.1 %shard_map.64 = bf16[128,4096]{1,0:T(8,128)(2,1)S(1)} custom-call(s32[8]{0:T(128)} %docs_hbm.1, s32[2,128]{1,0:T(2,128)} %bitcast.11, bf16[128,4096]{1,0:T(8,128)(2,1)} %bitcast.8, bf16[128,1024]{1,0:T(8,128)(2,1)} %bitcast.9, bf16[128,1024]{1,0:T(8,128)(2,1)} %bitcast.10, bf16[512,2048]{1,0:T(8,128)(2,1)} %bitcast.7), custom_call_target="tpu_custom_call" | custom-call | tf_op jit(solution)/shard_map/pallas_call | solution.py:476
  35.1 1.0 %copy.8 = bf16[1,128,4096]{2,1,0:T(8,128)(2,1)} copy(bf16[1,128,4096]{2,1,0:T(8,128)(2,1)S(1)} %bitcast.6) | data formatting | bytes 2097152
